TPU v7x, 32 devices: a whole 2x2x4 slice. The times are simulated.
32 devices in a mesh: py: 4 (over y, core), px: 2 (over x), pz: 4 (over z).
Axes of the slice: x: 2, y: 2, z: 4, core: 2. Of those that a mesh axis runs over, the one named last changes fastest.
Arguments:
- starting_state: float32 [512, 8, 128, 128], P('py', 'px', 'pz'), may hold values from 0.5 to 2
- scaled_conductivity: float32 [512, 8, 128, 128], P('py', 'px', 'pz'), may hold values from 0.03 to 0.15
- scaled_heat_supply: float32 [512, 8, 128, 128], P('py', 'px', 'pz'), may hold values from -0.2 to 0.2
Outputs:
- normalised_result: float32 [512, 8, 128, 128], P('py', 'px', 'pz')
- temperature_end: float32 [512, 8, 128, 128], P('py', 'px', 'pz')
All inputs are finite; a program needn't handle non-finite values.
Results may differ from a plain program's by a relative error of at most 0.00002.
Values sent between devices are 32-bit elements; how exact they have to be, the bound alone decides.
A program may use at most 128 MiB of HBM per device.

v0:
```python
import functools

import jax
import jax.numpy as jnp
from jax import lax
from jax.experimental import pallas as pl
from jax.experimental.pallas import tpu as pltpu
from jax.sharding import PartitionSpec as P

STEPS = 4
MESH = pl.DeviceIdType.MESH


def kernel(pieces, pair, *refs):
    if pair:
        (u_in, c_in, s_in, c, s, u, zh, sq, sqr,
         load, xs, xr, ys, yr, zs, zr, qs, qr) = refs
    else:
        (u_in, c_in, s_in, s, u, zh, c,
         load, xs, xr, ys, yr, zs, zr) = refs
    rows, width, height, lanes = c.shape
    size = rows // pieces
    half = pieces // 2

    names = ("py", "px", "pz")
    here = {name: lax.axis_index(name) for name in names}
    last = {name: lax.axis_size(name) - 1 for name in names}

    def has(name, side):
        return here[name] > 0 if side == 0 else here[name] < last[name]

    def beside(name, side):
        return {name: here[name] + (2 * side - 1)}

    def piece(p):
        odd = p % 2
        return half + (p // 2) * (1 - 2 * odd) - odd

    def span(k, pad=0):
        return pl.ds(k * size + pad, size)

    inner = pl.ds(1, width)

    def load_copy(which, k):
        if which == 0:
            return pltpu.make_async_copy(
                u_in.at[span(k)], u.at[0, span(k, 1), inner], load.at[0, k])
        src, dst = ((c_in, c), (s_in, s))[which - 1]
        return pltpu.make_async_copy(src.at[span(k)], dst.at[span(k)], load.at[which, k])

    def x_copy(slot, side, k, to):
        return pltpu.make_async_remote_copy(
            src_ref=u.at[slot, span(k, 1), pl.ds(width if side else 1, 1)],
            dst_ref=u.at[slot, span(k, 1), pl.ds(0 if side else width + 1, 1)],
            send_sem=xs.at[slot, side, k], recv_sem=xr.at[slot, 1 - side, k],
            device_id=beside("px", to), device_id_type=MESH)

    def z_copy(slot, side, k, to):
        return pltpu.make_async_remote_copy(
            src_ref=u.at[slot, span(k, 1), inner, pl.ds(height - 1 if side else 0, 1)],
            dst_ref=zh.at[slot, 1 - side, span(k)],
            send_sem=zs.at[slot, side, k], recv_sem=zr.at[slot, 1 - side, k],
            device_id=beside("pz", to), device_id_type=MESH)

    def y_copy(slot, side, to):
        return pltpu.make_async_remote_copy(
            src_ref=u.at[slot, pl.ds(rows if side else 1, 1), inner],
            dst_ref=u.at[slot, pl.ds(0 if side else rows + 1, 1), inner],
            send_sem=ys.at[slot, side], recv_sem=yr.at[slot, 1 - side],
            device_id=beside("py", to), device_id_type=MESH)

    def each_side(slot, k, act):
        for side in (0, 1):
            @pl.when(has("px", side))
            def _(side=side):
                act(lambda d, t: x_copy(slot, d, k, t), side)

            @pl.when(has("pz", side))
            def _(side=side):
                act(lambda d, t: z_copy(slot, d, k, t), side)

            edge = pieces - 1 if side else 0

            @pl.when(jnp.logical_and(has("py", side), k == edge))
            def _(side=side):
                act(lambda d, t: y_copy(slot, d, t), side)

    def send(slot, k):
        each_side(slot, k, lambda copy, side: copy(side, side).start())

    def sent(slot, k):
        each_side(slot, k, lambda copy, side: copy(side, side).wait_send())

    def arrived(slot, k):
        each_side(slot, k, lambda copy, side: copy(1 - side, side).wait_recv())

    def sums_copy(k):
        return pltpu.make_async_remote_copy(
            src_ref=sq.at[span(k)], dst_ref=sqr.at[span(k)],
            send_sem=qs.at[k], recv_sem=qr.at[k],
            device_id={"px": 1 - here["px"]}, device_id_type=MESH)

    def over_pieces(act):
        def one(p, carry):
            act(piece(p))
            return carry
        lax.fori_loop(0, pieces, one, 0)

    over_pieces(lambda k: load_copy(0, k).start())

    def load_rest(k):
        load_copy(1, k).start()
        load_copy(2, k).start()

    over_pieces(load_rest)

    barrier = pltpu.get_barrier_semaphore()
    count = 0
    for name in names:
        for side in (0, 1):
            there = has(name, side)
            count = count + there.astype(jnp.int32)

            @pl.when(there)
            def _(name=name, side=side):
                pl.semaphore_signal(
                    barrier, inc=1, device_id=beside(name, side), device_id_type=MESH)
    pl.semaphore_wait(barrier, count)

    def first_send(k):
        load_copy(0, k).wait()
        send(0, k)

    over_pieces(first_send)

    for side in (0, 1):
        for slot in (0, 1):
            @pl.when(jnp.logical_not(has("py", side)))
            def _(side=side, slot=slot):
                u[slot, rows + 1 if side else 0, 1:width + 1] = jnp.zeros(
                    (width, height, lanes), jnp.float32)

            @pl.when(jnp.logical_not(has("px", side)))
            def _(side=side, slot=slot):
                def clear(r, carry):
                    u[slot, r + 1, width + 1 if side else 0] = jnp.zeros(
                        (height, lanes), jnp.float32)
                    return carry
                lax.fori_loop(0, rows, clear, 0)

            @pl.when(jnp.logical_not(has("pz", side)))
            def _(side=side, slot=slot):
                def clear(r, carry):
                    zh[slot, side, r] = jnp.zeros((width, 1, lanes), jnp.float32)
                    return carry
                lax.fori_loop(0, rows, clear, 0)

    level = lax.broadcasted_iota(jnp.int32, (width, height, lanes), 1)

    for step in range(1, STEPS + 1):
        old, new = (step - 1) % 2, step % 2

        def row(r, old, new, final):
            centre = u[old, r + 1, 1:width + 1]
            below = jnp.where(
                level == 0, zh[old, 0, r], pltpu.roll(centre, 1, axis=1))
            above = jnp.where(
                level == height - 1, zh[old, 1, r], pltpu.roll(centre, height - 1, axis=1))
            spread = (
                u[old, r, 1:width + 1]
                + u[old, r + 2, 1:width + 1]
                + u[old, r + 1, 0:width]
                + u[old, r + 1, 2:width + 2]
                + below
                + above
                - 6.0 * centre
            )
            value = centre + c[r] * spread + s[r]
            if final:
                s[r] = value
            else:
                u[new, r + 1, 1:width + 1] = value
            if final and pair:
                mean = jnp.sum(value, axis=0) * (1.0 / width)
                apart = value - mean[None]
                sq[r, 0] = mean
                sq[r, 1] = jnp.sum(apart * apart, axis=0)

        def sweep(k, step=step, old=old, new=new):
            if step == 1:
                load_copy(1, k).wait()
                load_copy(2, k).wait()
            arrived(old, k)
            if 2 <= step < STEPS:
                sent(new, k)

            def one(i, carry):
                row(k * size + i, old, new, step == STEPS)
                return carry
            lax.fori_loop(0, size, one, 0)
            if step < STEPS:
                send(new, k)
            elif pair:
                sums_copy(k).start()

        over_pieces(sweep)

    def finish(k):
        sums_copy(k).wait_recv()

        def one(i, carry):
            r = k * size + i
            mine, other = sq[r, 0], sqr[r, 0]
            gap = mine - other
            mean = 0.5 * (mine + other)
            variance = (sq[r, 1] + sqr[r, 1]) * (0.5 / width) + 0.25 * gap * gap
            scale = lax.rsqrt(variance + 0.0001)
            c[r] = (s[r] - mean[None]) * scale[None]
            return carry
        lax.fori_loop(0, size, one, 0)

    def close(k):
        for slot in sorted({(STEPS - 1) % 2, (STEPS - 2) % 2}):
            sent(slot, k)
        if pair:
            sums_copy(k).wait_send()

    if pair:
        over_pieces(finish)
    over_pieces(close)


def put_out(pieces, count, *refs):
    held, out, done = refs[:count], refs[count:2 * count], refs[-1]
    size = held[0].shape[0] // pieces
    copies = [
        pltpu.make_async_copy(
            held[i].at[pl.ds(k * size, size)], out[i].at[pl.ds(k * size, size)], done.at[i, k])
        for k in range(pieces)
        for i in range(count)
    ]
    for copy in copies:
        copy.start()
    for copy in copies:
        copy.wait()


def body(starting_state, scaled_conductivity, scaled_heat_supply):
    rows, width, height, lanes = starting_state.shape
    pieces = next(n for n in (8, 4, 2) if rows % n == 0)
    pair = lax.axis_size("px") == 2
    dma = pltpu.SemaphoreType.DMA
    block = jax.ShapeDtypeStruct(starting_state.shape, jnp.float32)
    field = pltpu.VMEM((rows, width, height, lanes), jnp.float32)
    sums = pltpu.VMEM((rows, 2, height, lanes), jnp.float32)
    scratch = [
        pltpu.VMEM((2, rows + 2, width + 2, height, lanes), jnp.float32),
        pltpu.VMEM((2, 2, rows, width, 1, lanes), jnp.float32),
    ]
    scratch += [sums, sums] if pair else [field]
    scratch += [
        dma((3, pieces)),
        dma((2, 2, pieces)), dma((2, 2, pieces)),
        dma((2, 2)), dma((2, 2)),
        dma((2, 2, pieces)), dma((2, 2, pieces)),
    ]
    scratch += [dma((pieces,)), dma((pieces,))] if pair else []
    outputs = pl.pallas_call(
        functools.partial(kernel, pieces, pair),
        out_shape=(field, field) if pair else (field,),
        in_specs=[pl.BlockSpec(memory_space=pl.ANY)] * 3,
        out_specs=(pl.BlockSpec(memory_space=pltpu.VMEM),) * (2 if pair else 1),
        scratch_shapes=scratch,
        compiler_params=pltpu.CompilerParams(
            collective_id=0, has_side_effects=True, vmem_limit_bytes=(38 if pair else 40) * 1024 * 1024),
    )(starting_state, scaled_conductivity, scaled_heat_supply)
    outputs = pl.pallas_call(
        functools.partial(put_out, pieces, len(outputs)),
        out_shape=(block,) * len(outputs),
        in_specs=[pl.BlockSpec(memory_space=pltpu.VMEM)] * len(outputs),
        out_specs=(pl.BlockSpec(memory_space=pl.ANY),) * len(outputs),
        scratch_shapes=[dma((len(outputs), pieces))],
        compiler_params=pltpu.CompilerParams(vmem_limit_bytes=1024 * 1024),
    )(*outputs)
    if pair:
        return outputs
    (end,) = outputs
    line = width * lax.axis_size("px")
    guess = 1.0
    moved = end - guess
    totals, squares = lax.psum(
        (jnp.sum(moved, axis=1, keepdims=True), jnp.sum(moved * moved, axis=1, keepdims=True)), "px"
    )
    row_average = guess + totals / line
    line_variance = squares / line - totals / line * (totals / line)
    return ((end - row_average) * lax.rsqrt(line_variance + 0.0001), end)


def solution(mesh):
    placed = P("py", "px", "pz", None)
    return jax.shard_map(
        body,
        mesh=mesh,
        in_specs=(placed, placed, placed),
        out_specs=(placed, placed),
        check_vma=False,
    )
```

profile of v0, /device:TPU:1, one launch (start us, length us, event | category | flops | bytes accessed | tf_op | source)
XLA Modules:
  0.0 283.0 jit_solution(14368068783325988285)
XLA Ops:
  0.6 276.4 %shard_map.50 = (f32[128,4,32,128]{3,2,1,0:T(8,128)S(1)}, f32[128,4,32,128]{3,2,1,0:T(8,128)S(1)}) custom-call(f32[128,4,32,128]{3,2,1,0:T(8,128)} %refs_0_.1, f32[128,4,32,128]{3,2,1,0:T(8,128)} %refs_1_.1, f32[128,4,32,128]{3,2,1,0:T(8,128)} %refs_2_.1), custom_call_target="tpu_custom_call" | custom-call | tf_op jit(solution)/shard_map/pallas_call | solution.py:268
  277.0 6.0 %shard_map.51 = (f32[128,4,32,128]{3,2,1,0:T(8,128)}, f32[128,4,32,128]{3,2,1,0:T(8,128)}) custom-call(f32[128,4,32,128]{3,2,1,0:T(8,128)S(1)} %get-tuple-element.4.refs_0_, f32[128,4,32,128]{3,2,1,0:T(8,128)S(1)} %get-tuple-element.5.refs_1_), custom_call_target="tpu_custom_call" | custom-call | tf_op jit(solution)/shard_map/pallas_call | solution.py:277
where the time goes:
time: 284 us; the launch traced here: 283 us
  Pallas kernels  282 us (99%)
    pallas_call x1, Pallas kernels, body(): pl.pallas_call(functools.partial(kernel, pieces, pair), out_shape=(field,...  276 us
    pallas_call x1, Pallas kernels, body(): pl.pallas_call(functools.partial(put_out, pieces, len(outputs)), out_shap...  5.96 us

commit v1 on v0

--- a/solution.py
+++ b/solution.py
@@ -11,9 +11,31 @@
 MESH = pl.DeviceIdType.MESH
 
 
+def left_over(rows, pieces, turn):
+    size = rows // pieces
+    return (size, size) if turn == 0 else (max(size // 4, 1), 0)
+
+
+def cut_pieces(rows, pieces):
+    size = rows // pieces
+    cut = set()
+    for turn in (0, 1):
+        head, foot = left_over(rows, pieces, turn)
+        cut |= {k for k in range(pieces) if k * size < head or (k + 1) * size > rows - foot}
+    return sorted(cut)
+
+
+def normalise(mine, sums, others):
+    width = mine.shape[0]
+    gap = sums[0] - others[0]
+    mean = 0.5 * (sums[0] + others[0])
+    variance = (sums[1] + others[1]) * (0.5 / width) + 0.25 * gap * gap
+    return (mine - mean[None]) * lax.rsqrt(variance + 0.0001)[None]
+
+
 def kernel(pieces, pair, *refs):
     if pair:
-        (u_in, c_in, s_in, c, s, u, zh, sq, sqr,
+        (u_in, c_in, s_in, c, s, sq, u, zh, sqr,
          load, xs, xr, ys, yr, zs, zr, qs, qr) = refs
     else:
         (u_in, c_in, s_in, s, u, zh, c,
@@ -94,25 +116,35 @@
     def arrived(slot, k):
         each_side(slot, k, lambda copy, side: copy(1 - side, side).wait_recv())
 
-    def sums_copy(k):
+    def sums_copy(k, rows_of):
         return pltpu.make_async_remote_copy(
-            src_ref=sq.at[span(k)], dst_ref=sqr.at[span(k)],
+            src_ref=sq.at[rows_of], dst_ref=sqr.at[rows_of],
             send_sem=qs.at[k], recv_sem=qr.at[k],
             device_id={"px": 1 - here["px"]}, device_id_type=MESH)
+
+    def each_sum(k, act):
+        cut = jnp.bool_(False)
+        for e in cut_pieces(rows, pieces):
+            cut = jnp.logical_or(cut, k == e)
+
+        @pl.when(jnp.logical_not(cut))
+        def _():
+            act(sums_copy(k, span(k)), k * size, size)
+
+        for turn in (0, 1):
+            head, foot = left_over(rows, pieces, turn)
+            for e in cut_pieces(rows, pieces):
+                low, high = max(e * size, head), min((e + 1) * size, rows - foot)
+                if high > low:
+                    @pl.when(jnp.logical_and(k == e, here["py"] % 2 == turn))
+                    def _(e=e, low=low, high=high):
+                        act(sums_copy(e, pl.ds(low, high - low)), low, high - low)
 
     def over_pieces(act):
         def one(p, carry):
             act(piece(p))
             return carry
         lax.fori_loop(0, pieces, one, 0)
-
-    over_pieces(lambda k: load_copy(0, k).start())
-
-    def load_rest(k):
-        load_copy(1, k).start()
-        load_copy(2, k).start()
-
-    over_pieces(load_rest)
 
     barrier = pltpu.get_barrier_semaphore()
     count = 0
@@ -125,6 +157,15 @@
             def _(name=name, side=side):
                 pl.semaphore_signal(
                     barrier, inc=1, device_id=beside(name, side), device_id_type=MESH)
+
+    over_pieces(lambda k: load_copy(0, k).start())
+
+    def load_rest(k):
+        load_copy(1, k).start()
+        load_copy(2, k).start()
+
+    over_pieces(load_rest)
+
     pl.semaphore_wait(barrier, count)
 
     def first_send(k):
@@ -201,48 +242,123 @@
             if step < STEPS:
                 send(new, k)
             elif pair:
-                sums_copy(k).start()
+                each_sum(k, lambda copy, first, count: copy.start())
 
         over_pieces(sweep)
 
-    def finish(k):
-        sums_copy(k).wait_recv()
+    def finish(copy, first, count):
+        copy.wait_recv()
 
         def one(i, carry):
-            r = k * size + i
-            mine, other = sq[r, 0], sqr[r, 0]
-            gap = mine - other
-            mean = 0.5 * (mine + other)
-            variance = (sq[r, 1] + sqr[r, 1]) * (0.5 / width) + 0.25 * gap * gap
-            scale = lax.rsqrt(variance + 0.0001)
-            c[r] = (s[r] - mean[None]) * scale[None]
+            r = first + i
+            c[r] = normalise(s[r], sq[r], sqr[r])
             return carry
-        lax.fori_loop(0, size, one, 0)
+        lax.fori_loop(0, count, one, 0)
 
     def close(k):
         for slot in sorted({(STEPS - 1) % 2, (STEPS - 2) % 2}):
             sent(slot, k)
         if pair:
-            sums_copy(k).wait_send()
+            each_sum(k, lambda copy, first, count: copy.wait_send())
 
     if pair:
-        over_pieces(finish)
+        over_pieces(lambda k: each_sum(k, finish))
     over_pieces(close)
+
+
+def copy_all(copies):
+    for copy in copies:
+        copy.start()
+    for copy in copies:
+        copy.wait()
 
 
 def put_out(pieces, count, *refs):
     held, out, done = refs[:count], refs[count:2 * count], refs[-1]
     size = held[0].shape[0] // pieces
-    copies = [
+    copy_all([
         pltpu.make_async_copy(
             held[i].at[pl.ds(k * size, size)], out[i].at[pl.ds(k * size, size)], done.at[i, k])
         for k in range(pieces)
         for i in range(count)
-    ]
-    for copy in copies:
-        copy.start()
-    for copy in copies:
-        copy.wait()
+    ])
+
+
+def put_most(pieces, result, end, result_out, end_out, mark, done):
+    rows = end.shape[0]
+    size = rows // pieces
+    mark[...] = jnp.zeros(mark.shape, mark.dtype)
+    for turn in (0, 1):
+        @pl.when(lax.axis_index("py") % 2 == turn)
+        def _(turn=turn):
+            head, foot = left_over(rows, pieces, turn)
+            copies = []
+            for k in range(pieces):
+                whole = pl.ds(k * size, size)
+                copies.append(pltpu.make_async_copy(
+                    end.at[whole], end_out.at[whole], done.at[0, k]))
+                low, high = max(k * size, head), min((k + 1) * size, rows - foot)
+                if high > low:
+                    part = pl.ds(low, high - low)
+                    copies.append(pltpu.make_async_copy(
+                        result.at[part], result_out.at[part], done.at[1, k]))
+            copy_all(copies)
+
+
+def left_parts(rows, pieces, turn):
+    size = rows // pieces
+    head, foot = left_over(rows, pieces, turn)
+    parts = [(rows - foot + i, head + i, min(size, foot - i)) for i in range(0, foot, size)]
+    low = head
+    while low > 0:
+        count = min(size // 2, max(low // 2, size // 8, 1))
+        low -= count
+        parts.append((low, low, count))
+    return parts
+
+
+def exchange_rest(pieces, sums, end, mark, out, other, sent, got):
+    rows = end.shape[0]
+    partner = {"px": 1 - lax.axis_index("px")}
+    barrier = pltpu.get_barrier_semaphore()
+    pl.semaphore_signal(barrier, inc=1, device_id=partner, device_id_type=MESH)
+    pl.semaphore_wait(barrier, 1)
+    for turn in (0, 1):
+        @pl.when(lax.axis_index("py") % 2 == turn)
+        def _(turn=turn):
+            parts = left_parts(rows, pieces, turn)
+            copies = [
+                pltpu.make_async_remote_copy(
+                    src_ref=sums.at[pl.ds(row, count)], dst_ref=other.at[pl.ds(at, count)],
+                    send_sem=sent.at[n], recv_sem=got.at[n],
+                    device_id=partner, device_id_type=MESH)
+                for n, (row, at, count) in enumerate(parts)
+            ]
+            for copy in copies:
+                copy.start()
+            for copy, (row, at, count) in zip(copies, parts):
+                copy.wait_recv()
+
+                def one(i, carry, row=row, at=at):
+                    out[at + i] = normalise(end[row + i], sums[row + i], other[at + i])
+                    return carry
+                lax.fori_loop(0, count, one, 0)
+            for copy in copies:
+                copy.wait_send()
+
+
+def put_rest(pieces, rest, result, result_out, done):
+    rows = result.shape[0]
+    for turn in (0, 1):
+        @pl.when(lax.axis_index("py") % 2 == turn)
+        def _(turn=turn):
+            head, foot = left_over(rows, pieces, turn)
+            pairs = [((rows - foot, head), foot), ((0, 0), head)]
+            copy_all([
+                pltpu.make_async_copy(
+                    rest.at[pl.ds(at, count)], result_out.at[pl.ds(row, count)], done.at[n])
+                for n, ((row, at), count) in enumerate(pairs) if count
+            ])
 
 
 def body(starting_state, scaled_conductivity, scaled_heat_supply):
@@ -253,11 +369,12 @@
     block = jax.ShapeDtypeStruct(starting_state.shape, jnp.float32)
     field = pltpu.VMEM((rows, width, height, lanes), jnp.float32)
     sums = pltpu.VMEM((rows, 2, height, lanes), jnp.float32)
+    here, there = pl.BlockSpec(memory_space=pltpu.VMEM), pl.BlockSpec(memory_space=pl.ANY)
     scratch = [
         pltpu.VMEM((2, rows + 2, width + 2, height, lanes), jnp.float32),
         pltpu.VMEM((2, 2, rows, width, 1, lanes), jnp.float32),
     ]
-    scratch += [sums, sums] if pair else [field]
+    scratch += [sums] if pair else [field]
     scratch += [
         dma((3, pieces)),
         dma((2, 2, pieces)), dma((2, 2, pieces)),
@@ -265,25 +382,56 @@
         dma((2, 2, pieces)), dma((2, 2, pieces)),
     ]
     scratch += [dma((pieces,)), dma((pieces,))] if pair else []
+    made = (field, field, sums) if pair else (field,)
     outputs = pl.pallas_call(
         functools.partial(kernel, pieces, pair),
-        out_shape=(field, field) if pair else (field,),
-        in_specs=[pl.BlockSpec(memory_space=pl.ANY)] * 3,
-        out_specs=(pl.BlockSpec(memory_space=pltpu.VMEM),) * (2 if pair else 1),
+        out_shape=made,
+        in_specs=[there] * 3,
+        out_specs=(here,) * len(made),
         scratch_shapes=scratch,
         compiler_params=pltpu.CompilerParams(
-            collective_id=0, has_side_effects=True, vmem_limit_bytes=(38 if pair else 40) * 1024 * 1024),
+            collective_id=0, has_side_effects=True, vmem_limit_bytes=(34 if pair else 40) * 1024 * 1024),
     )(starting_state, scaled_conductivity, scaled_heat_supply)
+    if pair:
+        held, end, kept = outputs
+        result, end_out, mark = pl.pallas_call(
+            functools.partial(put_most, pieces),
+            out_shape=(block, block, pltpu.VMEM((8, 128), jnp.float32)),
+            in_specs=[here] * 2,
+            out_specs=(there, there, here),
+            scratch_shapes=[dma((2, pieces))],
+            compiler_params=pltpu.CompilerParams(vmem_limit_bytes=1024 * 1024),
+        )(held, end)
+        most = max(sum(left_over(rows, pieces, turn)) for turn in (0, 1))
+        parts = max(len(left_parts(rows, pieces, turn)) for turn in (0, 1))
+        rest = pl.pallas_call(
+            functools.partial(exchange_rest, pieces),
+            out_shape=pltpu.VMEM((most, width, height, lanes), jnp.float32),
+            in_specs=[here] * 3,
+            out_specs=here,
+            scratch_shapes=[
+                pltpu.VMEM((most, 2, height, lanes), jnp.float32), dma((parts,)), dma((parts,))],
+            compiler_params=pltpu.CompilerParams(
+                collective_id=1, has_side_effects=True, vmem_limit_bytes=4 * 1024 * 1024),
+        )(kept, end, mark)
+        result = pl.pallas_call(
+            functools.partial(put_rest, pieces),
+            out_shape=block,
+            in_specs=[here, there],
+            out_specs=there,
+            scratch_shapes=[dma((2,))],
+            input_output_aliases={1: 0},
+            compiler_params=pltpu.CompilerParams(vmem_limit_bytes=1024 * 1024),
+        )(rest, result)
+        return result, end_out
     outputs = pl.pallas_call(
         functools.partial(put_out, pieces, len(outputs)),
         out_shape=(block,) * len(outputs),
-        in_specs=[pl.BlockSpec(memory_space=pltpu.VMEM)] * len(outputs),
-        out_specs=(pl.BlockSpec(memory_space=pl.ANY),) * len(outputs),
+        in_specs=[here] * len(outputs),
+        out_specs=(there,) * len(outputs),
         scratch_shapes=[dma((len(outputs), pieces))],
         compiler_params=pltpu.CompilerParams(vmem_limit_bytes=1024 * 1024),
     )(*outputs)
-    if pair:
-        return outputs
     (end,) = outputs
     line = width * lax.axis_size("px")
     guess = 1.0

time: 284 us -> 279 us (0.982)
  Pallas kernels: 282 us -> 276 us
    pallas_call x2 -> x4, Pallas kernels: 282 us -> 276 us  [the longest x1 264 us: body(): pl.pallas_call(functools.partial(kernel, pieces, pair), out_shape=made, i...]
where the time goes in v1:
time: 279 us; the launch traced here: 277 us
  Pallas kernels  276 us (99%)
    pallas_call x1, Pallas kernels, body(): pl.pallas_call(functools.partial(kernel, pieces, pair), out_shape=made, i...  264 us
    pallas_call x1, Pallas kernels, body(): pl.pallas_call(functools.partial(put_most, pieces), out_shape=(block, blo...  5.95 us
    pallas_call x1, Pallas kernels, body(): pl.pallas_call(functools.partial(exchange_rest, pieces), out_shape=pltpu....  5.68 us

profile of v1, /device:TPU:1, one launch (start us, length us, event | category | flops | bytes accessed | tf_op | source)
XLA Modules:
  0.0 276.9 jit_solution(12669464744925116077)
XLA Ops:
  0.6 263.9 %shard_map.50 = (f32[128,4,32,128]{3,2,1,0:T(8,128)S(1)}, f32[128,4,32,128]{3,2,1,0:T(8,128)S(1)}, f32[128,2,32,128]{3,2,1,0:T(8,128)S(1)}) custom-call(f32[128,4,32,128]{3,2,1,0:T(8,128)} %refs_0_.1, f32[128,4,32,128]{3,2,1,0:T(8,128)} %refs_1_.1, f32[128,4,32,128]{3,2,1,0:T(8,128)} %refs_2_.1), custom_call_target="tpu_custom_call" | custom-call | tf_op jit(solution)/shard_map/pallas_call | solution.py:386
  264.5 5.9 %shard_map.51 = (f32[128,4,32,128]{3,2,1,0:T(8,128)}, f32[128,4,32,128]{3,2,1,0:T(8,128)}, f32[8,128]{1,0:T(8,128)S(1)}) custom-call(f32[128,4,32,128]{3,2,1,0:T(8,128)S(1)} %get-tuple-element.10.result, f32[128,4,32,128]{3,2,1,0:T(8,128)S(1)} %get-tuple-element.9.end), custom_call_target="tpu_custom_call" | custom-call | tf_op jit(solution)/shard_map/pallas_call | solution.py:397
  270.5 5.7 %shard_map.52.rest = f32[32,4,32,128]{3,2,1,0:T(8,128)S(1)} custom-call(f32[128,2,32,128]{3,2,1,0:T(8,128)S(1)} %get-tuple-element.8.sums, f32[128,4,32,128]{3,2,1,0:T(8,128)S(1)} %get-tuple-element.9.end, f32[8,128]{1,0:T(8,128)S(1)} %get-tuple-element.11.mark), custom_call_target="tpu_custom_call" | custom-call | tf_op jit(solution)/shard_map/pallas_call | solution.py:407
  276.2 0.7 shard_map.53

commit v2 on v1

--- a/solution.py
+++ b/solution.py
@@ -13,7 +13,7 @@
 
 def left_over(rows, pieces, turn):
     size = rows // pieces
-    return (size, size) if turn == 0 else (max(size // 4, 1), 0)
+    return (size, size) if turn == 1 else (0, 0)
 
 
 def cut_pieces(rows, pieces):
@@ -320,13 +320,16 @@
 def exchange_rest(pieces, sums, end, mark, out, other, sent, got):
     rows = end.shape[0]
     partner = {"px": 1 - lax.axis_index("px")}
-    barrier = pltpu.get_barrier_semaphore()
-    pl.semaphore_signal(barrier, inc=1, device_id=partner, device_id_type=MESH)
-    pl.semaphore_wait(barrier, 1)
     for turn in (0, 1):
+        parts = left_parts(rows, pieces, turn)
+        if not parts:
+            continue
+
         @pl.when(lax.axis_index("py") % 2 == turn)
-        def _(turn=turn):
-            parts = left_parts(rows, pieces, turn)
+        def _(parts=parts):
+            barrier = pltpu.get_barrier_semaphore()
+            pl.semaphore_signal(barrier, inc=1, device_id=partner, device_id_type=MESH)
+            pl.semaphore_wait(barrier, 1)
             copies = [
                 pltpu.make_async_remote_copy(
                     src_ref=sums.at[pl.ds(row, count)], dst_ref=other.at[pl.ds(at, count)],

time: 279 us -> 277 us (level)
    pallas_call x1, Pallas kernels: 264 us -> 254 us  [body(): pl.pallas_call(functools.partial(kernel, pieces, pair), out_shape=made, i...]
    pallas_call x1, Pallas kernels: 5.68 us -> 15.4 us  [body(): pl.pallas_call(functools.partial(exchange_rest, pieces), out_shape=pltpu....]
where the time goes in v2:
time: 277 us
  Pallas kernels  276 us (100%)
    pallas_call x1, Pallas kernels, body(): pl.pallas_call(functools.partial(kernel, pieces, pair), out_shape=made, i...  254 us
    pallas_call x1, Pallas kernels, body(): pl.pallas_call(functools.partial(exchange_rest, pieces), out_shape=pltpu....  15.4 us

profile of v2, /device:TPU:1, one launch (start us, length us, event | category | flops | bytes accessed | tf_op | source)
XLA Modules:
  0.0 276.6 jit_solution(2930446626564790283)
XLA Ops:
  0.6 253.8 %shard_map.50 = (f32[128,4,32,128]{3,2,1,0:T(8,128)S(1)}, f32[128,4,32,128]{3,2,1,0:T(8,128)S(1)}, f32[128,2,32,128]{3,2,1,0:T(8,128)S(1)}) custom-call(f32[128,4,32,128]{3,2,1,0:T(8,128)} %refs_0_.1, f32[128,4,32,128]{3,2,1,0:T(8,128)} %refs_1_.1, f32[128,4,32,128]{3,2,1,0:T(8,128)} %refs_2_.1), custom_call_target="tpu_custom_call" | custom-call | tf_op jit(solution)/shard_map/pallas_call | solution.py:389
  254.4 5.4 %shard_map.51 = (f32[128,4,32,128]{3,2,1,0:T(8,128)}, f32[128,4,32,128]{3,2,1,0:T(8,128)}, f32[8,128]{1,0:T(8,128)S(1)}) custom-call(f32[128,4,32,128]{3,2,1,0:T(8,128)S(1)} %get-tuple-element.10.result, f32[128,4,32,128]{3,2,1,0:T(8,128)S(1)} %get-tuple-element.9.end), custom_call_target="tpu_custom_call" | custom-call | tf_op jit(solution)/shard_map/pallas_call | solution.py:400
  259.8 15.4 %shard_map.52.rest = f32[32,4,32,128]{3,2,1,0:T(8,128)S(1)} custom-call(f32[128,2,32,128]{3,2,1,0:T(8,128)S(1)} %get-tuple-element.8.sums, f32[128,4,32,128]{3,2,1,0:T(8,128)S(1)} %get-tuple-element.9.end, f32[8,128]{1,0:T(8,128)S(1)} %get-tuple-element.11.mark), custom_call_target="tpu_custom_call" | custom-call | tf_op jit(solution)/shard_map/pallas_call | solution.py:410
  275.2 1.3 shard_map.53

commit v3 on v2

--- a/solution.py
+++ b/solution.py
@@ -70,9 +70,10 @@
         src, dst = ((c_in, c), (s_in, s))[which - 1]
         return pltpu.make_async_copy(src.at[span(k)], dst.at[span(k)], load.at[which, k])
 
-    def x_copy(slot, side, k, to):
+    def x_copy(slot, side, k, to, first=False):
+        inside = u_in.at[span(k), pl.ds(width - 1 if side else 0, 1)]
         return pltpu.make_async_remote_copy(
-            src_ref=u.at[slot, span(k, 1), pl.ds(width if side else 1, 1)],
+            src_ref=inside if first else u.at[slot, span(k, 1), pl.ds(width if side else 1, 1)],
             dst_ref=u.at[slot, span(k, 1), pl.ds(0 if side else width + 1, 1)],
             send_sem=xs.at[slot, side, k], recv_sem=xr.at[slot, 1 - side, k],
             device_id=beside("px", to), device_id_type=MESH)
@@ -91,16 +92,25 @@
             send_sem=ys.at[slot, side], recv_sem=yr.at[slot, 1 - side],
             device_id=beside("py", to), device_id_type=MESH)
 
-    def each_side(slot, k, act):
+    def each_side(slot, k, act, x=True, rest=(0, 1), met=False):
         for side in (0, 1):
-            @pl.when(has("px", side))
-            def _(side=side):
-                act(lambda d, t: x_copy(slot, d, k, t), side)
-
-            @pl.when(has("pz", side))
+            if x:
+                @pl.when(has("px", side))
+                def _(side=side):
+                    act(lambda d, t: x_copy(slot, d, k, t), side)
+
+            if side not in rest:
+                continue
+            beyond = has("pz", side)
+            if met and side == 1:
+                beyond = jnp.logical_and(beyond, k != half)
+
+            @pl.when(beyond)
             def _(side=side):
                 act(lambda d, t: z_copy(slot, d, k, t), side)
 
+            if met and side == 1:
+                continue
             edge = pieces - 1 if side else 0
 
             @pl.when(jnp.logical_and(has("py", side), k == edge))
@@ -113,8 +123,8 @@
     def sent(slot, k):
         each_side(slot, k, lambda copy, side: copy(side, side).wait_send())
 
-    def arrived(slot, k):
-        each_side(slot, k, lambda copy, side: copy(1 - side, side).wait_recv())
+    def arrived(slot, k, met):
+        each_side(slot, k, lambda copy, side: copy(1 - side, side).wait_recv(), met=met)
 
     def sums_copy(k, rows_of):
         return pltpu.make_async_remote_copy(
@@ -146,33 +156,55 @@
             return carry
         lax.fori_loop(0, pieces, one, 0)
 
+    load_copy(0, half).start()
     barrier = pltpu.get_barrier_semaphore()
     count = 0
-    for name in names:
-        for side in (0, 1):
-            there = has(name, side)
-            count = count + there.astype(jnp.int32)
-
-            @pl.when(there)
-            def _(name=name, side=side):
-                pl.semaphore_signal(
-                    barrier, inc=1, device_id=beside(name, side), device_id_type=MESH)
-
-    over_pieces(lambda k: load_copy(0, k).start())
+    for name, side in (("px", 0), ("px", 1), ("pz", 1), ("py", 1)):
+        there = has(name, side)
+        count = count + has(name, side if name == "px" else 0).astype(jnp.int32)
+
+        @pl.when(there)
+        def _(name=name, side=side):
+            pl.semaphore_signal(
+                barrier, inc=1, device_id=beside(name, side), device_id_type=MESH)
+
+    def after_first(act):
+        def one(p, carry):
+            act(piece(p))
+            return carry
+        lax.fori_loop(1, pieces, one, 0)
+
+    def start(copy, side):
+        copy(side, side).start()
+
+    def first_x(k):
+        load_copy(0, k).wait()
+        each_side(0, k, start, rest=())
 
     def load_rest(k):
         load_copy(1, k).start()
         load_copy(2, k).start()
 
+    pl.semaphore_wait(barrier, count)
+    for side in (0, 1):
+        @pl.when(has("px", side))
+        def _(side=side):
+            x_copy(0, side, half, side, first=True).start()
+    after_first(lambda k: load_copy(0, k).start())
+    load_copy(0, half).wait()
+    after_first(first_x)
     over_pieces(load_rest)
-
-    pl.semaphore_wait(barrier, count)
-
-    def first_send(k):
-        load_copy(0, k).wait()
-        send(0, k)
-
-    over_pieces(first_send)
+    over_pieces(lambda k: each_side(0, k, start, x=False, rest=(0,)))
+
+    @pl.when(has("pz", 1))
+    def _():
+        z_copy(0, 0, half, 1).wait_recv()
+        over_pieces(lambda k: z_copy(0, 1, k, 1).start())
+
+    @pl.when(has("py", 1))
+    def _():
+        y_copy(0, 0, 1).wait_recv()
+        y_copy(0, 1, 1).start()
 
     for side in (0, 1):
         for slot in (0, 1):
@@ -231,7 +263,7 @@
             if step == 1:
                 load_copy(1, k).wait()
                 load_copy(2, k).wait()
-            arrived(old, k)
+            arrived(old, k, step == 1)
             if 2 <= step < STEPS:
                 sent(new, k)
 

time: 277 us -> 276 us (level)
  no operation moved by 1% of the time
where the time goes in v3:
time: 276 us
  Pallas kernels  275 us (100%)
    pallas_call x1, Pallas kernels, body(): pl.pallas_call(functools.partial(kernel, pieces, pair), out_shape=made, i...  253 us
    pallas_call x1, Pallas kernels, body(): pl.pallas_call(functools.partial(exchange_rest, pieces), out_shape=pltpu....  14.9 us

profile of v3, /device:TPU:1, one launch (start us, length us, event | category | flops | bytes accessed | tf_op | source)
XLA Modules:
  0.0 275.7 jit_solution(7116511213784421197)
XLA Ops:
  0.6 253.4 %shard_map.50 = (f32[128,4,32,128]{3,2,1,0:T(8,128)S(1)}, f32[128,4,32,128]{3,2,1,0:T(8,128)S(1)}, f32[128,2,32,128]{3,2,1,0:T(8,128)S(1)}) custom-call(f32[128,4,32,128]{3,2,1,0:T(8,128)} %refs_0_.1, f32[128,4,32,128]{3,2,1,0:T(8,128)} %refs_1_.1, f32[128,4,32,128]{3,2,1,0:T(8,128)} %refs_2_.1), custom_call_target="tpu_custom_call" | custom-call | tf_op jit(solution)/shard_map/pallas_call | solution.py:421
  254.0 5.4 %shard_map.51 = (f32[128,4,32,128]{3,2,1,0:T(8,128)}, f32[128,4,32,128]{3,2,1,0:T(8,128)}, f32[8,128]{1,0:T(8,128)S(1)}) custom-call(f32[128,4,32,128]{3,2,1,0:T(8,128)S(1)} %get-tuple-element.10.result, f32[128,4,32,128]{3,2,1,0:T(8,128)S(1)} %get-tuple-element.9.end), custom_call_target="tpu_custom_call" | custom-call | tf_op jit(solution)/shard_map/pallas_call | solution.py:432
  259.4 14.9 %shard_map.52.rest = f32[32,4,32,128]{3,2,1,0:T(8,128)S(1)} custom-call(f32[128,2,32,128]{3,2,1,0:T(8,128)S(1)} %get-tuple-element.8.sums, f32[128,4,32,128]{3,2,1,0:T(8,128)S(1)} %get-tuple-element.9.end, f32[8,128]{1,0:T(8,128)S(1)} %get-tuple-element.11.mark), custom_call_target="tpu_custom_call" | custom-call | tf_op jit(solution)/shard_map/pallas_call | solution.py:442
  274.3 1.3 shard_map.53

commit v4 on v3

--- a/solution.py
+++ b/solution.py
@@ -68,14 +68,14 @@
             return pltpu.make_async_copy(
                 u_in.at[span(k)], u.at[0, span(k, 1), inner], load.at[0, k])
         src, dst = ((c_in, c), (s_in, s))[which - 1]
-        return pltpu.make_async_copy(src.at[span(k)], dst.at[span(k)], load.at[which, k])
+        return pltpu.make_async_copy(src, dst, load.at[1, which - 1])
 
     def x_copy(slot, side, k, to, first=False):
         inside = u_in.at[span(k), pl.ds(width - 1 if side else 0, 1)]
         return pltpu.make_async_remote_copy(
             src_ref=inside if first else u.at[slot, span(k, 1), pl.ds(width if side else 1, 1)],
             dst_ref=u.at[slot, span(k, 1), pl.ds(0 if side else width + 1, 1)],
-            send_sem=xs.at[slot, side, k], recv_sem=xr.at[slot, 1 - side, k],
+            send_sem=xs.at[slot, 0 if pair else side, k], recv_sem=xr.at[slot, 0 if pair else 1 - side, k],
             device_id=beside("px", to), device_id_type=MESH)
 
     def z_copy(slot, side, k, to):
@@ -181,10 +181,6 @@
         load_copy(0, k).wait()
         each_side(0, k, start, rest=())
 
-    def load_rest(k):
-        load_copy(1, k).start()
-        load_copy(2, k).start()
-
     pl.semaphore_wait(barrier, count)
     for side in (0, 1):
         @pl.when(has("px", side))
@@ -193,7 +189,8 @@
     after_first(lambda k: load_copy(0, k).start())
     load_copy(0, half).wait()
     after_first(first_x)
-    over_pieces(load_rest)
+    load_copy(1, 0).start()
+    load_copy(2, 0).start()
     over_pieces(lambda k: each_side(0, k, start, x=False, rest=(0,)))
 
     @pl.when(has("pz", 1))
@@ -260,9 +257,6 @@
                 sq[r, 1] = jnp.sum(apart * apart, axis=0)
 
         def sweep(k, step=step, old=old, new=new):
-            if step == 1:
-                load_copy(1, k).wait()
-                load_copy(2, k).wait()
             arrived(old, k, step == 1)
             if 2 <= step < STEPS:
                 sent(new, k)
@@ -276,6 +270,9 @@
             elif pair:
                 each_sum(k, lambda copy, first, count: copy.start())
 
+        if step == 1:
+            load_copy(1, 0).wait()
+            load_copy(2, 0).wait()
         over_pieces(sweep)
 
     def finish(copy, first, count):
@@ -343,7 +340,7 @@
     parts = [(rows - foot + i, head + i, min(size, foot - i)) for i in range(0, foot, size)]
     low = head
     while low > 0:
-        count = min(size // 2, max(low // 2, size // 8, 1))
+        count = min(low, size // 2, max(low // 2, size // 8, 1))
         low -= count
         parts.append((low, low, count))
     return parts
@@ -411,8 +408,8 @@
     ]
     scratch += [sums] if pair else [field]
     scratch += [
-        dma((3, pieces)),
-        dma((2, 2, pieces)), dma((2, 2, pieces)),
+        dma((2, pieces)),
+        dma((2, 1 if pair else 2, pieces)), dma((2, 1 if pair else 2, pieces)),
         dma((2, 2)), dma((2, 2)),
         dma((2, 2, pieces)), dma((2, 2, pieces)),
     ]

time: 276 us -> 276 us (level)
  no operation moved by 1% of the time
where the time goes in v4:
time: 276 us
  Pallas kernels  275 us (100%)
    pallas_call x1, Pallas kernels, body(): pl.pallas_call(functools.partial(kernel, pieces, pair), out_shape=made, i...  253 us
    pallas_call x1, Pallas kernels, body(): pl.pallas_call(functools.partial(exchange_rest, pieces), out_shape=pltpu....  15.3 us

profile of v4, /device:TPU:1, one launch (start us, length us, event | category | flops | bytes accessed | tf_op | source)
XLA Modules:
  0.0 275.7 jit_solution(10448552595842223803)
XLA Ops:
  0.6 253.0 %shard_map.50 = (f32[128,4,32,128]{3,2,1,0:T(8,128)S(1)}, f32[128,4,32,128]{3,2,1,0:T(8,128)S(1)}, f32[128,2,32,128]{3,2,1,0:T(8,128)S(1)}) custom-call(f32[128,4,32,128]{3,2,1,0:T(8,128)} %refs_0_.1, f32[128,4,32,128]{3,2,1,0:T(8,128)} %refs_1_.1, f32[128,4,32,128]{3,2,1,0:T(8,128)} %refs_2_.1), custom_call_target="tpu_custom_call" | custom-call | tf_op jit(solution)/shard_map/pallas_call | solution.py:418
  253.7 5.4 %shard_map.51 = (f32[128,4,32,128]{3,2,1,0:T(8,128)}, f32[128,4,32,128]{3,2,1,0:T(8,128)}, f32[8,128]{1,0:T(8,128)S(1)}) custom-call(f32[128,4,32,128]{3,2,1,0:T(8,128)S(1)} %get-tuple-element.10.result, f32[128,4,32,128]{3,2,1,0:T(8,128)S(1)} %get-tuple-element.9.end), custom_call_target="tpu_custom_call" | custom-call | tf_op jit(solution)/shard_map/pallas_call | solution.py:429
  259.0 15.3 %shard_map.52.rest = f32[32,4,32,128]{3,2,1,0:T(8,128)S(1)} custom-call(f32[128,2,32,128]{3,2,1,0:T(8,128)S(1)} %get-tuple-element.8.sums, f32[128,4,32,128]{3,2,1,0:T(8,128)S(1)} %get-tuple-element.9.end, f32[8,128]{1,0:T(8,128)S(1)} %get-tuple-element.11.mark), custom_call_target="tpu_custom_call" | custom-call | tf_op jit(solution)/shard_map/pallas_call | solution.py:439
  274.3 1.3 shard_map.53

commit v5 on v4

--- a/solution.py
+++ b/solution.py
@@ -156,7 +156,6 @@
             return carry
         lax.fori_loop(0, pieces, one, 0)
 
-    load_copy(0, half).start()
     barrier = pltpu.get_barrier_semaphore()
     count = 0
     for name, side in (("px", 0), ("px", 1), ("pz", 1), ("py", 1)):
@@ -186,7 +185,7 @@
         @pl.when(has("px", side))
         def _(side=side):
             x_copy(0, side, half, side, first=True).start()
-    after_first(lambda k: load_copy(0, k).start())
+    over_pieces(lambda k: load_copy(0, k).start())
     load_copy(0, half).wait()
     after_first(first_x)
     load_copy(1, 0).start()

time: 276 us -> 276 us (level)
  no operation moved by 1% of the time
where the time goes in v5:
time: 276 us
  Pallas kernels  275 us (100%)
    pallas_call x1, Pallas kernels, body(): pl.pallas_call(functools.partial(kernel, pieces, pair), out_shape=made, i...  253 us
    pallas_call x1, Pallas kernels, body(): pl.pallas_call(functools.partial(exchange_rest, pieces), out_shape=pltpu....  15.3 us

profile of v5, /device:TPU:1, one launch (start us, length us, event | category | flops | bytes accessed | tf_op | source)
XLA Modules:
  0.0 275.7 jit_solution(12520979626808775356)
XLA Ops:
  0.6 253.0 %shard_map.50 = (f32[128,4,32,128]{3,2,1,0:T(8,128)S(1)}, f32[128,4,32,128]{3,2,1,0:T(8,128)S(1)}, f32[128,2,32,128]{3,2,1,0:T(8,128)S(1)}) custom-call(f32[128,4,32,128]{3,2,1,0:T(8,128)} %refs_0_.1, f32[128,4,32,128]{3,2,1,0:T(8,128)} %refs_1_.1, f32[128,4,32,128]{3,2,1,0:T(8,128)} %refs_2_.1), custom_call_target="tpu_custom_call" | custom-call | tf_op jit(solution)/shard_map/pallas_call | solution.py:417
  253.7 5.4 %shard_map.51 = (f32[128,4,32,128]{3,2,1,0:T(8,128)}, f32[128,4,32,128]{3,2,1,0:T(8,128)}, f32[8,128]{1,0:T(8,128)S(1)}) custom-call(f32[128,4,32,128]{3,2,1,0:T(8,128)S(1)} %get-tuple-element.10.result, f32[128,4,32,128]{3,2,1,0:T(8,128)S(1)} %get-tuple-element.9.end), custom_call_target="tpu_custom_call" | custom-call | tf_op jit(solution)/shard_map/pallas_call | solution.py:428
  259.1 15.3 %shard_map.52.rest = f32[32,4,32,128]{3,2,1,0:T(8,128)S(1)} custom-call(f32[128,2,32,128]{3,2,1,0:T(8,128)S(1)} %get-tuple-element.8.sums, f32[128,4,32,128]{3,2,1,0:T(8,128)S(1)} %get-tuple-element.9.end, f32[8,128]{1,0:T(8,128)S(1)} %get-tuple-element.11.mark), custom_call_target="tpu_custom_call" | custom-call | tf_op jit(solution)/shard_map/pallas_call | solution.py:438
  274.3 1.3 shard_map.53

commit v6 on v4

--- a/solution.py
+++ b/solution.py
@@ -109,11 +109,14 @@
             def _(side=side):
                 act(lambda d, t: z_copy(slot, d, k, t), side)
 
-            if met and side == 1:
+            if rest != (0, 1):
                 continue
             edge = pieces - 1 if side else 0
-
-            @pl.when(jnp.logical_and(has("py", side), k == edge))
+            beyond = jnp.logical_and(has("py", side), k == edge)
+            if met:
+                beyond = jnp.logical_and(beyond, patient)
+
+            @pl.when(beyond)
             def _(side=side):
                 act(lambda d, t: y_copy(slot, d, t), side)
 
@@ -159,9 +162,14 @@
     load_copy(0, half).start()
     barrier = pltpu.get_barrier_semaphore()
     count = 0
-    for name, side in (("px", 0), ("px", 1), ("pz", 1), ("py", 1)):
+    patient = here["py"] % 2 == 0
+    for name, side in (("px", 0), ("px", 1), ("pz", 1), ("py", 0), ("py", 1)):
         there = has(name, side)
-        count = count + has(name, side if name == "px" else 0).astype(jnp.int32)
+        heard = has(name, 0 if name == "pz" else side)
+        if name == "py":
+            there, heard = (jnp.logical_and(there, jnp.logical_not(patient)),
+                            jnp.logical_and(heard, patient))
+        count = count + heard.astype(jnp.int32)
 
         @pl.when(there)
         def _(name=name, side=side):
@@ -192,16 +200,21 @@
     load_copy(1, 0).start()
     load_copy(2, 0).start()
     over_pieces(lambda k: each_side(0, k, start, x=False, rest=(0,)))
+    for side in (0, 1):
+        @pl.when(jnp.logical_and(has("py", side), patient))
+        def _(side=side):
+            y_copy(0, side, side).start()
 
     @pl.when(has("pz", 1))
     def _():
         z_copy(0, 0, half, 1).wait_recv()
         over_pieces(lambda k: z_copy(0, 1, k, 1).start())
 
-    @pl.when(has("py", 1))
-    def _():
-        y_copy(0, 0, 1).wait_recv()
-        y_copy(0, 1, 1).start()
+    for side in (0, 1):
+        @pl.when(jnp.logical_and(has("py", side), jnp.logical_not(patient)))
+        def _(side=side):
+            y_copy(0, 1 - side, side).wait_recv()
+            y_copy(0, side, side).start()
 
     for side in (0, 1):
         for slot in (0, 1):

time: 276 us -> 275 us (level)
  no operation moved by 1% of the time
where the time goes in v6:
time: 275 us
  Pallas kernels  274 us (100%)
    pallas_call x1, Pallas kernels, body(): pl.pallas_call(functools.partial(kernel, pieces, pair), out_shape=made, i...  252 us
    pallas_call x1, Pallas kernels, body(): pl.pallas_call(functools.partial(exchange_rest, pieces), out_shape=pltpu....  15.9 us

profile of v6, /device:TPU:1, one launch (start us, length us, event | category | flops | bytes accessed | tf_op | source)
XLA Modules:
  0.0 275.1 jit_solution(17174594586023474329)
XLA Ops:
  0.6 251.8 %shard_map.50 = (f32[128,4,32,128]{3,2,1,0:T(8,128)S(1)}, f32[128,4,32,128]{3,2,1,0:T(8,128)S(1)}, f32[128,2,32,128]{3,2,1,0:T(8,128)S(1)}) custom-call(f32[128,4,32,128]{3,2,1,0:T(8,128)} %refs_0_.1, f32[128,4,32,128]{3,2,1,0:T(8,128)} %refs_1_.1, f32[128,4,32,128]{3,2,1,0:T(8,128)} %refs_2_.1), custom_call_target="tpu_custom_call" | custom-call | tf_op jit(solution)/shard_map/pallas_call | solution.py:431
  252.5 5.4 %shard_map.51 = (f32[128,4,32,128]{3,2,1,0:T(8,128)}, f32[128,4,32,128]{3,2,1,0:T(8,128)}, f32[8,128]{1,0:T(8,128)S(1)}) custom-call(f32[128,4,32,128]{3,2,1,0:T(8,128)S(1)} %get-tuple-element.10.result, f32[128,4,32,128]{3,2,1,0:T(8,128)S(1)} %get-tuple-element.9.end), custom_call_target="tpu_custom_call" | custom-call | tf_op jit(solution)/shard_map/pallas_call | solution.py:442
  257.8 15.9 %shard_map.52.rest = f32[32,4,32,128]{3,2,1,0:T(8,128)S(1)} custom-call(f32[128,2,32,128]{3,2,1,0:T(8,128)S(1)} %get-tuple-element.8.sums, f32[128,4,32,128]{3,2,1,0:T(8,128)S(1)} %get-tuple-element.9.end, f32[8,128]{1,0:T(8,128)S(1)} %get-tuple-element.11.mark), custom_call_target="tpu_custom_call" | custom-call | tf_op jit(solution)/shard_map/pallas_call | solution.py:452
  273.7 1.3 shard_map.53
